TPU v7x, 32 devices: a whole 2x2x4 slice. The times are simulated.
32 devices in a mesh: dp: 8 (over y, x, core), tensor: 4 (over z).
Axes of the slice: x: 2, y: 2, z: 4, core: 2. Of those that a mesh axis runs over, the one named last changes fastest.
Arguments:
- layer_input: bfloat16 [1024, 8, 2048], P('tensor', 'dp'), may hold values from -6 to 6
- first_gain: bfloat16 [2048], replicated, may hold values from 0.25 to 1.75
- query_weight: bfloat16 [2048, 2048], P('dp', 'tensor'), may hold values from -0.125 to 0.125
- key_matrix: bfloat16 [2048, 1024], P('dp', 'tensor'), may hold values from -0.125 to 0.125
- value_matrix: bfloat16 [2048, 1024], P('dp', 'tensor'), may hold values from -0.125 to 0.125
- query_gain: bfloat16 [128], replicated, may hold values from 0.6 to 7
- key_gain: bfloat16 [128], replicated, may hold values from 0.6 to 7
- output_weight: bfloat16 [2048, 2048], P('dp', 'tensor'), may hold values from -0.75 to 0.75
- second_gain: bfloat16 [2048], replicated, may hold values from 0.25 to 1.75
- gate_weight: bfloat16 [2048, 6144], P('dp', 'tensor'), may hold values from -0.125 to 0.125
- up_weight: bfloat16 [2048, 6144], P('dp', 'tensor'), may hold values from -0.125 to 0.125
- down_weight: bfloat16 [2048, 6144], P('dp', 'tensor'), may hold values from -0.078125 to 0.078125
- segments: int32 [8, 1024], P('dp'), may hold values from 0 to 3, never falling along the last dimension, each value on 1 to 512 neighbouring positions
- cotangent: bfloat16 [1024, 8, 2048], P('tensor', 'dp'), may hold values from -6 to 6
Outputs:
- layer_output: bfloat16 [1024, 8, 2048], P('tensor', 'dp')
- input_grad: bfloat16 [1024, 8, 2048], P('tensor', 'dp')
- first_gain_grad: float32 [2048], replicated
- query_weight_grad: float32 [2048, 2048], P('dp', 'tensor')
- key_weight_grad: float32 [2048, 1024], P('dp', 'tensor')
- value_weight_grad: float32 [2048, 1024], P('dp', 'tensor')
- query_gain_grad: float32 [128], replicated
- key_gain_grad: float32 [128], replicated
- output_weight_grad: float32 [2048, 2048], P('dp', 'tensor')
- second_gain_grad: float32 [2048], replicated
- gate_weight_grad: float32 [2048, 6144], P('dp', 'tensor')
- up_weight_grad: float32 [2048, 6144], P('dp', 'tensor')
- down_weight_grad: float32 [2048, 6144], P('dp', 'tensor')
Inputs may be any that keep to these rules, and one draw needn't show every extreme that they name: `segments`: along each sequence the segment numbers never fall; every number appears, each document holds 1 to 512 positions and one holds exactly 512.
All inputs are finite; a program needn't handle non-finite values.
Results may differ from a plain program's by a relative error of at most 0.025.
The roundings to bfloat16 on the way count: a program that leaves them out, or rounds other values in their place, can miss the bound.
Values may be sent and summed in bfloat16 or wider, within the bound.
A program may use at most 192 MiB of HBM per device.

v0:
```python
import jax
import jax.numpy as jnp
from jax import lax
from jax.sharding import PartitionSpec as P

epsilon = 1e-06
rope_base = 1000000.0


def rms_parts(values, gain):
    inverse = lax.rsqrt(jnp.mean(values * values, axis=-1, keepdims=True) + epsilon)
    return (values * inverse * gain, inverse)


def rms_back(values, inverse, gain, upstream):
    normed = values * inverse
    inner_term = upstream * gain
    value_grad = inverse * (
        inner_term - normed * jnp.mean(inner_term * normed, axis=-1, keepdims=True)
    )
    return (value_grad, upstream * normed)


def rope_tables(sequence_length, head_size):
    half_width = head_size // 2
    frequency = rope_base ** (-(2.0 * jnp.arange(half_width, dtype=jnp.float32)) / head_size)
    angles = jnp.arange(sequence_length, dtype=jnp.float32)[:, None] * frequency[None, :]
    angles = jnp.concatenate([angles, angles], axis=1)
    return (jnp.cos(angles), jnp.sin(angles))


def rotate(values, cosine_table, sine_table):
    half_width = values.shape[-1] // 2
    turned = jnp.concatenate([-values[..., half_width:], values[..., :half_width]], axis=-1)
    return values * cosine_table + turned * sine_table


def rotate_back(upstream, cosine_table, sine_table):
    half_width = upstream.shape[-1] // 2
    shifted = upstream * sine_table
    return upstream * cosine_table + jnp.concatenate(
        [shifted[..., half_width:], -shifted[..., :half_width]], axis=-1
    )


def allowed_pairs(segment_row):
    position = jnp.arange(segment_row.shape[0])
    return (segment_row[:, None] == segment_row[None, :]) & (position[None, :] <= position[:, None])


def masked_scores(query_row_block, key_rows, allowed):
    factor = query_row_block.shape[-1] ** (-0.5)
    scores = (
        jnp.einsum("qhgd,khd->hgqk", query_row_block, key_rows, preferred_element_type=jnp.float32)
        * factor
    )
    return jnp.where(allowed, scores, -1e30)


def attend_forward(query_row_block, key_rows, value_rows, allowed):
    scores = masked_scores(query_row_block, key_rows, allowed)
    row_max = jnp.max(scores, axis=-1, keepdims=True)
    weights = jnp.exp(scores - row_max)
    row_total = jnp.sum(weights, axis=-1, keepdims=True)
    attention = (weights / row_total).astype(jnp.bfloat16)
    out_rows = jnp.einsum(
        "hgqk,khd->qhgd", attention, value_rows, preferred_element_type=jnp.float32
    )
    return (out_rows, row_max + jnp.log(row_total))


def attend_backward(query_row_block, key_rows, value_rows, allowed, log_total, grad_out):
    scores = masked_scores(query_row_block, key_rows, allowed)
    attention = jnp.exp(scores - log_total)
    grad_attention = jnp.einsum(
        "qhgd,khd->hgqk", grad_out, value_rows, preferred_element_type=jnp.float32
    )
    row_delta = jnp.sum(attention * grad_attention, axis=-1, keepdims=True)
    grad_scores = (attention * (grad_attention - row_delta)).astype(jnp.bfloat16)
    factor = query_row_block.shape[-1] ** (-0.5)
    grad_query = (
        jnp.einsum("hgqk,khd->qhgd", grad_scores, key_rows, preferred_element_type=jnp.float32)
        * factor
    )
    grad_key = (
        jnp.einsum(
            "hgqk,qhgd->khd", grad_scores, query_row_block, preferred_element_type=jnp.float32
        )
        * factor
    )
    grad_value = jnp.einsum(
        "hgqk,qhgd->khd",
        attention.astype(jnp.bfloat16),
        grad_out,
        preferred_element_type=jnp.float32,
    )
    return (
        grad_query.astype(jnp.bfloat16),
        grad_key.astype(jnp.bfloat16),
        grad_value.astype(jnp.bfloat16),
    )


def fetch_attention(query_weight, key_matrix, value_matrix, output_weight):
    return (
        lax.all_gather(query_weight, "dp", axis=0, tiled=True),
        lax.all_gather(key_matrix, "dp", axis=0, tiled=True),
        lax.all_gather(value_matrix, "dp", axis=0, tiled=True),
        lax.all_gather(output_weight, "dp", axis=0, tiled=True),
    )


def fetch_feedforward(gate_weight, up_weight, down_weight):
    return (
        lax.all_gather(gate_weight, "dp", axis=0, tiled=True),
        lax.all_gather(up_weight, "dp", axis=0, tiled=True),
        lax.all_gather(down_weight, "dp", axis=0, tiled=True),
    )


def gather_rows(values):
    return lax.all_gather(values, "tensor", axis=0, tiled=True)


def gather_cotangent(values):
    return lax.all_gather(values, "tensor", axis=0, tiled=True)


def branch_total(term_fn, short_rows):
    return lax.psum_scatter(
        term_fn(jnp.int32(0), short_rows * lax.axis_size("tensor")).astype(jnp.bfloat16),
        "tensor",
        scatter_dimension=0,
        tiled=True,
    ).astype(jnp.float32)


def input_total(term_fn, short_rows):
    return lax.psum_scatter(
        term_fn(jnp.int32(0), short_rows * lax.axis_size("tensor")).astype(jnp.bfloat16),
        "tensor",
        scatter_dimension=0,
        tiled=True,
    ).astype(jnp.float32)


def project_rows(left, right):
    return jnp.einsum("lsc,dc->lsd", left, right, preferred_element_type=jnp.float32)


def weight_term(rows_in, grads_in):
    return jnp.einsum("lsd,lsc->dc", rows_in, grads_in, preferred_element_type=jnp.float32)


def body(
    layer_input,
    first_gain,
    query_weight,
    key_matrix,
    value_matrix,
    query_gain,
    key_gain,
    output_weight,
    second_gain,
    gate_weight,
    up_weight,
    down_weight,
    segments,
    cotangent,
):
    short_rows = layer_input.shape[0]
    sequence_length = short_rows * lax.axis_size("tensor")
    seq_count = layer_input.shape[1]
    head_size = query_gain.shape[0]
    kv_heads = key_matrix.shape[1] // head_size
    query_heads = query_weight.shape[1] // head_size
    head_groups = query_heads // kv_heads
    cosine_table, sine_table = rope_tables(sequence_length, head_size)
    cos_heads = cosine_table[:, None, None, :]
    sin_heads = sine_table[:, None, None, :]
    gain_one = first_gain.astype(jnp.float32)
    gain_two = second_gain.astype(jnp.float32)
    gain_query = query_gain.astype(jnp.float32)
    gain_key = key_gain.astype(jnp.float32)
    query_full, key_full, value_full, output_full = fetch_attention(
        query_weight, key_matrix, value_matrix, output_weight
    )
    source = layer_input.astype(jnp.float32)
    first_normalized, inverse_one = rms_parts(source, gain_one)
    rows_one = gather_rows(first_normalized.astype(jnp.bfloat16))
    proj_query = jnp.einsum("lsd,dc->lsc", rows_one, query_full, preferred_element_type=jnp.float32)
    proj_query = proj_query.reshape(sequence_length, seq_count, query_heads, head_size)
    projected_key = jnp.einsum(
        "lsd,dc->lsc", rows_one, key_full, preferred_element_type=jnp.float32
    )
    projected_key = projected_key.reshape(sequence_length, seq_count, kv_heads, head_size)
    projected_value = jnp.einsum(
        "lsd,dc->lsc", rows_one, value_full, preferred_element_type=jnp.float32
    )
    projected_value = projected_value.reshape(sequence_length, seq_count, kv_heads, head_size)
    unit_query, inverse_query = rms_parts(proj_query, gain_query)
    unit_key, inverse_key = rms_parts(projected_key, gain_key)
    query_row_block = rotate(unit_query, cos_heads, sin_heads).astype(jnp.bfloat16)
    key_rows = rotate(unit_key, cos_heads, sin_heads).astype(jnp.bfloat16)
    value_rows = projected_value.astype(jnp.bfloat16)
    member = 0
    allowed = allowed_pairs(segments[member])
    out_rows, log_total = attend_forward(
        query_row_block[:, member].reshape(sequence_length, kv_heads, head_groups, head_size),
        key_rows[:, member],
        value_rows[:, member],
        allowed,
    )
    attended_list = [out_rows.reshape(sequence_length, query_heads * head_size)]
    log_totals = [log_total]
    masks = [allowed]
    attended = jnp.stack(attended_list, axis=1).astype(jnp.bfloat16)
    branch = branch_total(
        lambda row_start, row_count: project_rows(attended, output_full), short_rows
    )
    middle = source + branch
    gate_complete, up_complete, down_complete = fetch_feedforward(
        gate_weight, up_weight, down_weight
    )
    normed_two, inverse_two = rms_parts(middle, gain_two)
    second_rows = gather_rows(normed_two.astype(jnp.bfloat16))
    gate_projected = jnp.einsum(
        "qpt,to->qpo", second_rows, gate_complete, preferred_element_type=jnp.float32
    )
    up_projected = jnp.einsum(
        "qpt,to->qpo", second_rows, up_complete, preferred_element_type=jnp.float32
    )
    sigmoid_gate = jax.nn.sigmoid(gate_projected)
    activated = gate_projected * sigmoid_gate
    hidden = (activated * up_projected).astype(jnp.bfloat16)
    mixed = branch_total(
        lambda row_start, row_count: project_rows(hidden, down_complete), short_rows
    )
    layer_output = (middle + mixed).astype(jnp.bfloat16)
    gate_complete, up_complete, down_complete = fetch_feedforward(
        gate_weight, up_weight, down_weight
    )
    gradient_rows = gather_cotangent(cotangent)
    grad_hidden = jnp.einsum(
        "qpt,to->qpo", gradient_rows, down_complete, preferred_element_type=jnp.float32
    )
    down_grad = weight_term(gradient_rows, hidden)
    grad_gate = (
        grad_hidden * up_projected * sigmoid_gate * (1.0 + gate_projected * (1.0 - sigmoid_gate))
    ).astype(jnp.bfloat16)
    grad_up = (grad_hidden * activated).astype(jnp.bfloat16)
    gate_grad = weight_term(second_rows, grad_gate)
    up_grad = weight_term(second_rows, grad_up)
    grad_two = input_total(
        lambda row_start, row_count: project_rows(grad_gate, gate_complete)
        + project_rows(grad_up, up_complete),
        short_rows,
    )
    grad_mid_norm, gain_two_terms = rms_back(middle, inverse_two, gain_two, grad_two)
    grad_middle = cotangent.astype(jnp.float32) + grad_mid_norm
    query_full, key_full, value_full, output_full = fetch_attention(
        query_weight, key_matrix, value_matrix, output_weight
    )
    branch_rows = gather_cotangent(grad_middle.astype(jnp.bfloat16))
    grad_attended = jnp.einsum(
        "lsd,dc->lsc", branch_rows, output_full, preferred_element_type=jnp.float32
    ).astype(jnp.bfloat16)
    output_grad = weight_term(branch_rows, attended)
    member = 0
    grad_query, grad_key, grad_value = attend_backward(
        query_row_block[:, member].reshape(sequence_length, kv_heads, head_groups, head_size),
        key_rows[:, member],
        value_rows[:, member],
        masks[member],
        log_totals[member],
        grad_attended[:, member].reshape(sequence_length, kv_heads, head_groups, head_size),
    )
    query_list = [grad_query.reshape(sequence_length, query_heads, head_size)]
    key_list = [grad_key]
    value_list = [grad_value]
    grad_query_rows = jnp.stack(query_list, axis=1).astype(jnp.float32)
    grad_key_rows = jnp.stack(key_list, axis=1).astype(jnp.float32)
    grad_value_low = jnp.stack(value_list, axis=1).reshape(
        sequence_length, seq_count, kv_heads * head_size
    )
    grad_proj_query, query_gain_terms = rms_back(
        proj_query, inverse_query, gain_query, rotate_back(grad_query_rows, cos_heads, sin_heads)
    )
    grad_proj_key, key_gain_terms = rms_back(
        projected_key, inverse_key, gain_key, rotate_back(grad_key_rows, cos_heads, sin_heads)
    )
    grad_query_low = grad_proj_query.reshape(
        sequence_length, seq_count, query_heads * head_size
    ).astype(jnp.bfloat16)
    grad_key_low = grad_proj_key.reshape(sequence_length, seq_count, kv_heads * head_size).astype(
        jnp.bfloat16
    )
    query_grad = weight_term(rows_one, grad_query_low)
    key_grad = weight_term(rows_one, grad_key_low)
    value_grad = weight_term(rows_one, grad_value_low)
    grad_one = input_total(
        lambda row_start, row_count: project_rows(grad_query_low, query_full)
        + project_rows(grad_key_low, key_full)
        + project_rows(grad_value_low, value_full),
        short_rows,
    )
    grad_src_norm, gain_one_terms = rms_back(source, inverse_one, gain_one, grad_one)
    input_grad = (grad_middle + grad_src_norm).astype(jnp.bfloat16)
    gain_sums = lax.psum(
        (
            jnp.sum(gain_one_terms, axis=(0, 1)),
            jnp.sum(gain_two_terms, axis=(0, 1)),
            jnp.sum(query_gain_terms, axis=(0, 1, 2)),
            jnp.sum(key_gain_terms, axis=(0, 1, 2)),
        ),
        ("dp", "tensor"),
    )
    weight_sums = (
        lax.psum_scatter(
            query_grad.astype(jnp.bfloat16), "dp", scatter_dimension=0, tiled=True
        ).astype(jnp.float32),
        lax.psum_scatter(
            key_grad.astype(jnp.bfloat16), "dp", scatter_dimension=0, tiled=True
        ).astype(jnp.float32),
        lax.psum_scatter(
            value_grad.astype(jnp.bfloat16), "dp", scatter_dimension=0, tiled=True
        ).astype(jnp.float32),
        lax.psum_scatter(
            output_grad.astype(jnp.bfloat16), "dp", scatter_dimension=0, tiled=True
        ).astype(jnp.float32),
        lax.psum_scatter(
            gate_grad.astype(jnp.bfloat16), "dp", scatter_dimension=0, tiled=True
        ).astype(jnp.float32),
        lax.psum_scatter(
            up_grad.astype(jnp.bfloat16), "dp", scatter_dimension=0, tiled=True
        ).astype(jnp.float32),
        lax.psum_scatter(
            down_grad.astype(jnp.bfloat16), "dp", scatter_dimension=0, tiled=True
        ).astype(jnp.float32),
    )
    return (
        layer_output,
        input_grad,
        gain_sums[0],
        weight_sums[0],
        weight_sums[1],
        weight_sums[2],
        gain_sums[2],
        gain_sums[3],
        weight_sums[3],
        gain_sums[1],
        weight_sums[4],
        weight_sums[5],
        weight_sums[6],
    )


def solution(mesh):
    return jax.shard_map(
        body,
        mesh=mesh,
        in_specs=(
            P("tensor", "dp", None),
            P(),
            P("dp", "tensor"),
            P("dp", "tensor"),
            P("dp", "tensor"),
            P(),
            P(),
            P("dp", "tensor"),
            P(),
            P("dp", "tensor"),
            P("dp", "tensor"),
            P("dp", "tensor"),
            P("dp", None),
            P("tensor", "dp", None),
        ),
        out_specs=(
            P("tensor", "dp", None),
            P("tensor", "dp", None),
            P(),
            P("dp", "tensor"),
            P("dp", "tensor"),
            P("dp", "tensor"),
            P(),
            P(),
            P("dp", "tensor"),
            P(),
            P("dp", "tensor"),
            P("dp", "tensor"),
            P("dp", "tensor"),
        ),
        check_vma=False,
    )
```

profile of v0, /device:TPU:0, one launch (start us, length us, event | category | flops | bytes accessed | tf_op | source)
XLA Modules:
  0.0 1326.5 jit_solution(12982953722708710317)
XLA Ops:
  19.7 16.4 %all-gather.14.cloned.1.call-done = bf16[2048,256]{1,0:T(8,128)(2,1)} async-done(((bf16[256,256]{1,0:T(8,128)(2,1)}), bf16[2048,256]{1,0:T(8,128)(2,1)}) %all-gather.14.cloned.1.call-update) | async-done | bytes 1048592 | tf_op jit(solution)/shard_map/all_gather | solution.py:108
  38.3 23.0 %all-gather.16.cloned.1.call-done = bf16[2048,256]{1,0:T(8,128)(2,1)} async-done(((bf16[256,256]{1,0:T(8,128)(2,1)}), bf16[2048,256]{1,0:T(8,128)(2,1)}) %all-gather.16.cloned.1.call-update) | async-done | bytes 1048592 | tf_op jit(solution)/shard_map/all_gather | solution.py:107
  61.3 82.9 %all-gather.12.cloned.1.call-done = bf16[1024,1,2048]{2,0,1:T(8,128)(2,1)} async-done(((bf16[256,1,2048]{2,0,1:T(8,128)(2,1)}), bf16[1024,1,2048]{2,0,1:T(8,128)(2,1)}) %all-gather.12.cloned.1.call-update) | async-done | bytes 4194320 | tf_op jit(solution)/shard_map/all_gather | solution.py:122
  149.5 22.8 %all-gather.18.cloned.1.call-done = bf16[2048,512]{1,0:T(8,128)(2,1)} async-done(((bf16[256,512]{1,0:T(8,128)(2,1)}), bf16[2048,512]{1,0:T(8,128)(2,1)}) %all-gather.18.cloned.1.call-update) | async-done | bytes 2097168 | tf_op jit(solution)/shard_map/all_gather | solution.py:106
  192.7 8.0 fusion.3
  216.2 76.4 %reduce-scatter.12.cloned.1.call-done = bf16[256,1,2048]{2,0,1:T(8,128)(2,1)} async-done(((bf16[1024,1,2048]{2,0,1:T(8,128)(2,1)}), bf16[256,1,2048]{2,0,1:T(8,128)(2,1)}) %reduce-scatter.12.cloned.1.call-update) | async-done | bytes 1048592 | tf_op jit(solution)/shard_map/reduce_scatter | solution.py:130
  298.9 41.5 %all-gather.26.cloned.1.call-done = bf16[2048,1536]{1,0:T(8,128)(2,1)} async-done(((bf16[256,1536]{1,0:T(8,128)(2,1)}), bf16[2048,1536]{1,0:T(8,128)(2,1)}) %all-gather.26.cloned.1.call-update) | async-done | bytes 6291472 | tf_op jit(solution)/shard_map/all_gather | solution.py:116
  340.4 82.9 %all-gather.22.cloned.1.call-done = bf16[1024,1,2048]{2,0,1:T(8,128)(2,1)} async-done(((bf16[256,1,2048]{2,0,1:T(8,128)(2,1)}), bf16[1024,1,2048]{2,0,1:T(8,128)(2,1)}) %all-gather.22.cloned.1.call-update) | async-done | bytes 4194320 | tf_op jit(solution)/shard_map/all_gather | solution.py:122
  423.3 11.9 fusion.21
  435.2 33.9 %all-gather.24.cloned.1.call-done = bf16[2048,1536]{1,0:T(8,128)(2,1)} async-done(((bf16[256,1536]{1,0:T(8,128)(2,1)}), bf16[2048,1536]{1,0:T(8,128)(2,1)}) %all-gather.24.cloned.1.call-update) | async-done | bytes 6291472 | tf_op jit(solution)/shard_map/all_gather | solution.py:115
  469.1 11.8 fusion.23
  480.9 70.4 %all-gather.30.cloned.1.call-done = bf16[1024,1,2048]{2,0,1:T(8,128)(2,1)} async-done(((bf16[256,1,2048]{2,0,1:T(8,128)(2,1)}), bf16[1024,1,2048]{2,0,1:T(8,128)(2,1)}) %all-gather.30.cloned.1.call-update) | async-done | bytes 4194320 | tf_op jit(solution)/shard_map/all_gather | solution.py:126
  551.3 45.8 %all-gather.28.cloned.1.call-done = bf16[2048,1536]{1,0:T(8,128)(2,1)} async-done(((bf16[256,1536]{1,0:T(8,128)(2,1)}), bf16[2048,1536]{1,0:T(8,128)(2,1)}) %all-gather.28.cloned.1.call-update) | async-done | bytes 6291472 | tf_op jit(solution)/shard_map/all_gather | solution.py:117
  597.1 16.8 %multiply_convert_fusion = (bf16[1024,1536]{1,0:T(8,128)(2,1)}, bf16[1024,1536]{1,0:T(8,128)(2,1)S(1)}, bf16[1024,1536]{1,0:T(8,128)(2,1)}) fusion(f32[1024,1536]{1,0:T(8,128)} %fusion.23, f32[1024,1536]{1,0:T(8,128)} %fusion.21, bf16[2048,1536]{1,0:T(8,128)(2,1)} %all-gather.28.cloned.1.call-done, bf16[1024,1,2048]{2,0,1:T(8,128)(2,1)} %all-gather.30.cloned.1.call-done), kind=kOutput, calls=%fused_computation.20 | convolution fusion | flops 6466043904 | bytes 32505856 | tf_op jit(solution)/shard_map/qpt,to->qpo/dot_general | solution.py:244
  620.6 11.1 fusion.11
  631.8 76.9 %reduce-scatter.16.cloned.1.call-done = bf16[256,1,2048]{2,0,1:T(8,128)(2,1)} async-done(((bf16[1024,1,2048]{2,0,1:T(8,128)(2,1)}), bf16[256,1,2048]{2,0,1:T(8,128)(2,1)}) %reduce-scatter.16.cloned.1.call-update) | async-done | bytes 1048592 | tf_op jit(solution)/shard_map/reduce_scatter | solution.py:139
  713.1 11.4 fusion.9
  724.6 12.2 convolution_convert_fusion.1
  736.8 11.4 convolution_convert_fusion.2
  748.5 45.9 %all-gather.32.cloned.1.call-done = bf16[1024,1,2048]{2,0,1:T(8,128)(2,1)} async-done(((bf16[256,1,2048]{2,0,1:T(8,128)(2,1)}), bf16[1024,1,2048]{2,0,1:T(8,128)(2,1)}) %all-gather.32.cloned.1.call-update) | async-done | bytes 4194320 | tf_op jit(solution)/shard_map/all_gather | solution.py:126
  799.7 11.1 fusion.89
  822.0 8.3 fusion.2
  878.4 11.2 convert_bitcast_fusion
  892.2 30.6 %reduce-scatter.30.cloned.1.call-done = bf16[256,1536]{1,0:T(8,128)(2,1)} async-done(((bf16[2048,1536]{1,0:T(8,128)(2,1)}), bf16[256,1536]{1,0:T(8,128)(2,1)}) %reduce-scatter.30.cloned.1.call-update) | async-done | bytes 786448 | tf_op jit(solution)/shard_map/reduce_scatter | solution.py:334
  925.3 62.6 %reduce-scatter.28.cloned.1.call-done = bf16[256,1536]{1,0:T(8,128)(2,1)} async-done(((bf16[2048,1536]{1,0:T(8,128)(2,1)}), bf16[256,1536]{1,0:T(8,128)(2,1)}) %reduce-scatter.28.cloned.1.call-update) | async-done | bytes 786448 | tf_op jit(solution)/shard_map/reduce_scatter | solution.py:331
  990.3 36.6 %reduce-scatter.24.cloned.1.call-done = bf16[256,256]{1,0:T(8,128)(2,1)} async-done(((bf16[2048,256]{1,0:T(8,128)(2,1)}), bf16[256,256]{1,0:T(8,128)(2,1)}) %reduce-scatter.24.cloned.1.call-update) | async-done | bytes 131088 | tf_op jit(solution)/shard_map/reduce_scatter | solution.py:325
  1028.5 37.4 %reduce-scatter.22.cloned.1.call-done = bf16[256,256]{1,0:T(8,128)(2,1)} async-done(((bf16[2048,256]{1,0:T(8,128)(2,1)}), bf16[256,256]{1,0:T(8,128)(2,1)}) %reduce-scatter.22.cloned.1.call-update) | async-done | bytes 131088 | tf_op jit(solution)/shard_map/reduce_scatter | solution.py:322
  1067.5 42.8 %reduce-scatter.26.cloned.1.call-done = bf16[256,512]{1,0:T(8,128)(2,1)} async-done(((bf16[2048,512]{1,0:T(8,128)(2,1)}), bf16[256,512]{1,0:T(8,128)(2,1)}) %reduce-scatter.26.cloned.1.call-update) | async-done | bytes 262160 | tf_op jit(solution)/shard_map/reduce_scatter | solution.py:328
  1112.1 42.5 %reduce-scatter.20.cloned.1.call-done = bf16[256,512]{1,0:T(8,128)(2,1)} async-done(((bf16[2048,512]{1,0:T(8,128)(2,1)}), bf16[256,512]{1,0:T(8,128)(2,1)}) %reduce-scatter.20.cloned.1.call-update) | async-done | bytes 262160 | tf_op jit(solution)/shard_map/reduce_scatter | solution.py:319
  1156.4 77.3 %reduce-scatter.18.cloned.1.call-done = bf16[256,1,2048]{2,0,1:T(8,128)(2,1)} async-done(((bf16[1024,1,2048]{2,0,1:T(8,128)(2,1)}), bf16[256,1,2048]{2,0,1:T(8,128)(2,1)}) %reduce-scatter.18.cloned.1.call-update) | async-done | bytes 1048592 | tf_op jit(solution)/shard_map/reduce_scatter | solution.py:139
  1235.8 46.5 %all-reduce = (f32[2048]{0:T(1024)}, f32[128]{0:T(128)}, f32[128]{0:T(128)}, f32[2048]{0:T(1024)}) all-reduce(f32[2048]{0:T(1024)S(1)} %get-tuple-element.30, f32[128]{0:T(128)S(1)} %get-tuple-element.26, f32[128]{0:T(128)S(1)} %get-tuple-element.32, f32[2048]{0:T(1024)S(1)} %get-tuple-element.28), channel_id=1, replica_groups=mesh['dp'=8,'tensor'=4] {'dp','tensor'}, use_global_device_ids=true, to_apply=%region_16.17 | all-reduce | flops 4352 | bytes 34816 | tf_op jit(solution)/shard_map/psum | solution.py:309
  1282.3 32.1 %reduce-scatter.14.cloned.1.call-done = bf16[256,1,2048]{2,0,1:T(8,128)(2,1)} async-done(((bf16[1024,1,2048]{2,0,1:T(8,128)(2,1)}), bf16[256,1,2048]{2,0,1:T(8,128)(2,1)}) %reduce-scatter.14.cloned.1.call-update) | async-done | bytes 1048592 | tf_op jit(solution)/shard_map/reduce_scatter | solution.py:130
  (251 shorter events, 158.4 us)
Async XLA Ops:
  7.2 28.8 %all-gather.14.cloned.1.call-start = ((), (), s32[]{:S(2)}) async-start(), calls=%async_computation.12 | async-start | bytes 1179648 | tf_op jit(solution)/shard_map/all_gather | solution.py:108
  7.9 53.4 %all-gather.16.cloned.1.call-start = ((), (), s32[]{:S(2)}) async-start(), calls=%async_computation.13 | async-start | bytes 1179648 | tf_op jit(solution)/shard_map/all_gather | solution.py:107
  8.7 135.5 %all-gather.12.cloned.1.call-start = ((), (), s32[]{:S(2)}) async-start(), calls=%async_computation.11 | async-start | bytes 5242880 | tf_op jit(solution)/shard_map/all_gather | solution.py:122
  14.0 158.2 %all-gather.18.cloned.1.call-start = ((), (), s32[]{:S(2)}) async-start(), calls=%async_computation.14 | async-start | bytes 2359296 | tf_op jit(solution)/shard_map/all_gather | solution.py:106
  14.6 193.8 %all-gather.20.cloned.1.call-start = ((), (), s32[]{:S(2)}) async-start(), calls=%async_computation.15 | async-start | bytes 2359296 | tf_op jit(solution)/shard_map/all_gather | solution.py:109
  15.2 277.4 %reduce-scatter.12.cloned.1.call-start = ((), (), s32[]{:S(2)}) async-start(), calls=%async_computation.16 | async-start | bytes 5242880 | tf_op jit(solution)/shard_map/reduce_scatter | solution.py:130
  15.3 165.0 %copy-start.51 = (f32[128]{0:T(128)}, f32[128]{0:T(128)S(1)}, u32[]{:S(2)}) copy-start(f32[128]{0:T(128)S(1)} %convert_element_type.245) | copy-start | bytes 1540
  15.3 163.4 %copy-start.53 = (f32[128]{0:T(128)}, f32[128]{0:T(128)S(1)}, u32[]{:S(2)}) copy-start(f32[128]{0:T(128)S(1)} %convert_element_type.243) | copy-start | bytes 1540
  148.0 30.7 %copy-start.4 = (f32[1024,256]{0,1:T(8,128)}, f32[1024,256]{0,1:T(8,128)S(1)}, u32[]{:S(2)}) copy-start(f32[1024,256]{0,1:T(8,128)S(1)} %fusion.33) | copy-start | bytes 3145732
  215.4 77.2 %copy-start.3 = (bf16[256,1,2048]{2,0,1:T(8,128)(2,1)S(1)}, bf16[256,1,2048]{2,0,1:T(8,128)(2,1)}, u32[]{:S(2)}) copy-start(bf16[256,1,2048]{2,0,1:T(8,128)(2,1)} %param.14) | copy-start | bytes 3145732
  215.4 125.0 %all-gather.26.cloned.1.call-start = ((), (), s32[]{:S(2)}) async-start(), calls=%async_computation.19 | async-start | bytes 7077888 | tf_op jit(solution)/shard_map/all_gather | solution.py:116
  216.1 207.2 %all-gather.22.cloned.1.call-start = ((), (), s32[]{:S(2)}) async-start(), calls=%async_computation.17 | async-start | bytes 5242880 | tf_op jit(solution)/shard_map/all_gather | solution.py:122
  296.8 172.3 %all-gather.24.cloned.1.call-start = ((), (), s32[]{:S(2)}) async-start(), calls=%async_computation.18 | async-start | bytes 7077888 | tf_op jit(solution)/shard_map/all_gather | solution.py:115
  297.6 253.7 %all-gather.30.cloned.1.call-start = ((), (), s32[]{:S(2)}) async-start(), calls=%async_computation.22 | async-start | bytes 5242880 | tf_op jit(solution)/shard_map/all_gather | solution.py:126
  298.2 298.9 %all-gather.28.cloned.1.call-start = ((), (), s32[]{:S(2)}) async-start(), calls=%async_computation.20 | async-start | bytes 7077888 | tf_op jit(solution)/shard_map/all_gather | solution.py:117
  298.9 409.8 %reduce-scatter.16.cloned.1.call-start = ((), (), s32[]{:S(2)}) async-start(), calls=%async_computation.23 | async-start | bytes 5242880 | tf_op jit(solution)/shard_map/reduce_scatter | solution.py:139
  631.8 77.0 %copy-start.8 = (bf16[256,1,2048]{2,0,1:T(8,128)(2,1)S(1)}, bf16[256,1,2048]{2,0,1:T(8,128)(2,1)}, u32[]{:S(2)}) copy-start(bf16[256,1,2048]{2,0,1:T(8,128)(2,1)} %reduce-scatter.12.cloned.1.call-done) | copy-start | bytes 3145732
  631.8 79.2 %copy-start.19 = (bf16[256,1,2048]{2,0,1:T(8,128)(2,1)S(1)}, bf16[256,1,2048]{2,0,1:T(8,128)(2,1)}, u32[]{:S(2)}) copy-start(bf16[256,1,2048]{2,0,1:T(8,128)(2,1)} %param.27) | copy-start | bytes 3145732
  631.8 162.7 %all-gather.32.cloned.1.call-start = ((), (), s32[]{:S(2)}) async-start(), calls=%async_computation.24 | async-start | bytes 5242880 | tf_op jit(solution)/shard_map/all_gather | solution.py:126
  713.1 176.5 %reduce-scatter.32.cloned.1.call-start = ((), (), s32[]{:S(2)}) async-start(), calls=%async_computation.32 | async-start | bytes 7077888 | tf_op jit(solution)/shard_map/reduce_scatter | solution.py:337
  724.5 198.3 %reduce-scatter.30.cloned.1.call-start = ((), (), s32[]{:S(2)}) async-start(), calls=%async_computation.31 | async-start | bytes 7077888 | tf_op jit(solution)/shard_map/reduce_scatter | solution.py:334
  736.7 251.1 %reduce-scatter.28.cloned.1.call-start = ((), (), s32[]{:S(2)}) async-start(), calls=%async_computation.30 | async-start | bytes 7077888 | tf_op jit(solution)/shard_map/reduce_scatter | solution.py:331
  748.3 278.6 %reduce-scatter.24.cloned.1.call-start = ((), (), s32[]{:S(2)}) async-start(), calls=%async_computation.28 | async-start | bytes 1179648 | tf_op jit(solution)/shard_map/reduce_scatter | solution.py:325
  838.8 227.1 %reduce-scatter.22.cloned.1.call-start = ((), (), s32[]{:S(2)}) async-start(), calls=%async_computation.27 | async-start | bytes 1179648 | tf_op jit(solution)/shard_map/reduce_scatter | solution.py:322
  845.8 264.6 %reduce-scatter.26.cloned.1.call-start = ((), (), s32[]{:S(2)}) async-start(), calls=%async_computation.29 | async-start | bytes 2359296 | tf_op jit(solution)/shard_map/reduce_scatter | solution.py:328
  852.2 302.4 %reduce-scatter.20.cloned.1.call-start = ((), (), s32[]{:S(2)}) async-start(), calls=%async_computation.26 | async-start | bytes 2359296 | tf_op jit(solution)/shard_map/reduce_scatter | solution.py:319
  869.8 363.9 %reduce-scatter.18.cloned.1.call-start = ((), (), s32[]{:S(2)}) async-start(), calls=%async_computation.25 | async-start | bytes 5242880 | tf_op jit(solution)/shard_map/reduce_scatter | solution.py:139
  878.3 436.1 %reduce-scatter.14.cloned.1.call-start = ((), (), s32[]{:S(2)}) async-start(), calls=%async_computation.21 | async-start | bytes 5242880 | tf_op jit(solution)/shard_map/reduce_scatter | solution.py:130
  892.2 341.6 %copy-start.47 = (f32[2048]{0:T(1024)S(1)}, f32[2048]{0:T(1024)}, u32[]{:S(2)}) copy-start(f32[2048]{0:T(1024)} %copy-done.46) | copy-start | bytes 24580
  892.2 341.6 %copy-start.50 = (f32[256]{0:T(256)S(1)}, f32[256]{0:T(256)}, u32[]{:S(2)}) copy-start(f32[256]{0:T(256)} %copy-done.49) | copy-start | bytes 3076
  925.3 389.1 %copy-start.9 = (bf16[256,1,2048]{2,0,1:T(8,128)(2,1)S(1)}, bf16[256,1,2048]{2,0,1:T(8,128)(2,1)}, u32[]{:S(2)}) copy-start(bf16[256,1,2048]{2,0,1:T(8,128)(2,1)} %reduce-scatter.12.cloned.1.call-done) | copy-start | bytes 3145732
  925.3 389.1 %copy-start.20 = (bf16[256,1,2048]{2,0,1:T(8,128)(2,1)S(1)}, bf16[256,1,2048]{2,0,1:T(8,128)(2,1)}, u32[]{:S(2)}) copy-start(bf16[256,1,2048]{2,0,1:T(8,128)(2,1)} %param.27) | copy-start | bytes 3145732
  (57 other events, 241.4 us)
Sparse Core Ops, SparseCore 0:
  9.9 26.0 all-gather.13
  37.9 23.3 all-gather.15
  63.5 80.7 all-gather.11
  146.0 26.2 all-gather.17
  174.0 27.7 all-gather.19
  215.5 77.0 reduce-scatter.11
  294.4 45.9 all-gather.25
  342.5 80.7 all-gather.21
  425.2 43.8 all-gather.23
  470.5 80.7 all-gather.29
  553.2 43.8 all-gather.27
  631.9 76.7 reduce-scatter.15
  713.2 81.2 all-gather.31
  797.7 60.0 reduce-scatter.31
  861.0 61.7 reduce-scatter.29
  926.0 61.7 reduce-scatter.27
  990.9 35.9 reduce-scatter.23
  1029.9 35.9 reduce-scatter.21
  1069.2 41.1 reduce-scatter.25
  1113.5 41.1 reduce-scatter.19
  1156.9 76.7 reduce-scatter.17
  1236.0 78.3 reduce-scatter.13
where the time goes:
time: 1340 us; the launch traced here: 1330 us
  waiting for transfers between devices  986 us (74%)
  matrix products  192 us (14%)
  other arithmetic  62.4 us (5%)
  blocking collectives  46.5 us (3%)
  local copies, waits for them, and re-layouts  22.1 us (2%)
  between operations  15.7 us (1%)
    all_gather x2, waiting for transfers between devices, gather_rows(): return lax.all_gather(values, 'tensor', axis=0, tiled=True)  166 us
    reduce_scatter x2, waiting for transfers between devices, input_total(): lax.psum_scatter(term_fn(jnp.int32(0), short_rows * lax.axis_size('tensor...  154 us
    all_gather x2, waiting for transfers between devices, gather_cotangent(): return lax.all_gather(values, 'tensor', axis=0, tiled=True)  116 us
    reduce_scatter x2, waiting for transfers between devices, branch_total(): lax.psum_scatter(term_fn(jnp.int32(0), short_rows * lax.axis_size('tensor...  108 us
    reduce_scatter x1, waiting for transfers between devices, body(): lax.psum_scatter(gate_grad.astype(jnp.bfloat16), 'dp', scatter_dimension=...  62.6 us
    dot_general x7, matrix products, weight_term(): jnp.einsum('lsd,lsc->dc', rows_in, grads_in, preferred_element_type=jnp.f...  49.8 us
    psum x1, blocking collectives, body(): lax.psum((jnp.sum(gain_one_terms, axis=(0, 1)), jnp.sum(gain_two_terms, a...  46.5 us
    all_gather x1, waiting for transfers between devices, fetch_feedforward(): lax.all_gather(down_weight, 'dp', axis=0, tiled=True)  45.8 us
  transfers between devices with their start and end apart: 22, of which 20 were waited for; matrix products, arithmetic and copies ran while one was open for 16% of the time, Pallas kernels for 0%

commit v1 on v0

--- a/solution.py
+++ b/solution.py
@@ -5,6 +5,27 @@
 
 epsilon = 1e-06
 rope_base = 1000000.0
+
+
+def feed_the_columns(x_local):
+    mesh_dim = "tensor"
+    main, outcome_arr, v1 = (lax.axis_size(mesh_dim), lax.axis_index(mesh_dim), x_local.shape[0])
+    u1 = lax.dynamic_update_slice_in_dim(
+        jnp.zeros(
+            [j0 * main if k == 0 else j0 for k, j0 in enumerate(x_local.shape)], x_local.dtype
+        ),
+        x_local,
+        outcome_arr * v1,
+        axis=0,
+    )
+    answer = w1 = x_local
+    for at in range(1, main // 2 + 1):
+        answer = lax.ppermute(answer, mesh_dim, [(k, (k + 1) % main) for k in range(main)])
+        u1 = lax.dynamic_update_slice_in_dim(u1, answer, (outcome_arr - at) % main * v1, axis=0)
+        if 2 * at < main:
+            w1 = lax.ppermute(w1, mesh_dim, [(k, (k - 1) % main) for k in range(main)])
+            u1 = lax.dynamic_update_slice_in_dim(u1, w1, (outcome_arr + at) % main * v1, axis=0)
+    return u1
 
 
 def rms_parts(values, gain):
@@ -123,7 +144,7 @@
 
 
 def gather_cotangent(values):
-    return lax.all_gather(values, "tensor", axis=0, tiled=True)
+    return feed_the_columns(values)
 
 
 def branch_total(term_fn, short_rows):

time: 1340 us -> 1190 us (0.89)
  waiting for transfers between devices: 986 us -> 781 us
  starting transfers between devices: 1.52 us -> 49.7 us
    all_gather x2 -> x0, waiting for transfers between devices: 116 us -> none  [gather_cotangent(): return lax.all_gather(values, 'tensor', axis=0, tiled=True)]
    ppermute x0 -> x6, waiting for transfers between devices: none -> 104 us  [the longest x4 102 us: feed_the_columns(): lax.ppermute(answer, mesh_dim, [(k, (k + 1) % main) for k in range(main)])]
    reduce_scatter x1, waiting for transfers between devices: 62.6 us -> 0.02 us  [body(): lax.psum_scatter(gate_grad.astype(jnp.bfloat16), 'dp', scatter_dimension=...]
    ppermute x0 -> x6, starting transfers between devices: none -> 48.1 us  [the longest x4 43.4 us: feed_the_columns(): lax.ppermute(answer, mesh_dim, [(k, (k + 1) % main) for k in range(main)])]
    all_gather x1, waiting for transfers between devices: 41.5 us -> 0.01 us  [fetch_feedforward(): lax.all_gather(up_weight, 'dp', axis=0, tiled=True)]
    reduce_scatter x2, waiting for transfers between devices: 154 us -> 119 us  [input_total(): lax.psum_scatter(term_fn(jnp.int32(0), short_rows * lax.axis_size('tensor...]
    all_gather x2, waiting for transfers between devices: 166 us -> 133 us  [gather_rows(): return lax.all_gather(values, 'tensor', axis=0, tiled=True)]
    reduce_scatter x1, waiting for transfers between devices: 30.6 us -> 0.01 us  [body(): lax.psum_scatter(up_grad.astype(jnp.bfloat16), 'dp', scatter_dimension=0,...]
  transfers between devices with their start and end apart: 22 -> 26, of which waited for: 20 -> 21; matrix products, arithmetic and copies ran while one was open for 16% -> 19% of each run, Pallas kernels for 0% -> 0%
where the time goes in v1:
time: 1190 us; the launch traced here: 1180 us
  waiting for transfers between devices  781 us (66%)
  matrix products  191 us (16%)
  other arithmetic  65.7 us (6%)
  starting transfers between devices  49.7 us (4%)
  blocking collectives  46.4 us (4%)
  local copies, waits for them, and re-layouts  30.8 us (3%)
  between operations  15.6 us (1%)
    all_gather x2, waiting for transfers between devices, gather_rows(): return lax.all_gather(values, 'tensor', axis=0, tiled=True)  133 us
    reduce_scatter x2, waiting for transfers between devices, input_total(): lax.psum_scatter(term_fn(jnp.int32(0), short_rows * lax.axis_size('tensor...  119 us
    reduce_scatter x2, waiting for transfers between devices, branch_total(): lax.psum_scatter(term_fn(jnp.int32(0), short_rows * lax.axis_size('tensor...  108 us
    ppermute x4, waiting for transfers between devices, feed_the_columns(): lax.ppermute(answer, mesh_dim, [(k, (k + 1) % main) for k in range(main)])  102 us
    dot_general x7, matrix products, weight_term(): jnp.einsum('lsd,lsc->dc', rows_in, grads_in, preferred_element_type=jnp.f...  49.2 us
    psum x1, blocking collectives, body(): lax.psum((jnp.sum(gain_one_terms, axis=(0, 1)), jnp.sum(gain_two_terms, a...  46.4 us
    dot_general x7, matrix products, project_rows(): jnp.einsum('lsc,dc->lsd', left, right, preferred_element_type=jnp.float32)  44.6 us
    ppermute x4, starting transfers between devices, feed_the_columns(): lax.ppermute(answer, mesh_dim, [(k, (k + 1) % main) for k in range(main)])  43.4 us
  transfers between devices with their start and end apart: 26, of which 21 were waited for; matrix products, arithmetic and copies ran while one was open for 19% of the time, Pallas kernels for 0%

profile of v1, /device:TPU:0, one launch (start us, length us, event | category | flops | bytes accessed | tf_op | source)
XLA Modules:
  0.0 1179.6 jit_solution(1215502734976418746)
XLA Ops:
  19.1 16.9 %all-gather.12.cloned.1.call-done = bf16[2048,256]{1,0:T(8,128)(2,1)} async-done(((bf16[256,256]{1,0:T(8,128)(2,1)}), bf16[2048,256]{1,0:T(8,128)(2,1)}) %all-gather.12.cloned.1.call-update) | async-done | bytes 1048592 | tf_op jit(solution)/shard_map/all_gather | solution.py:129
  38.3 23.0 %all-gather.14.cloned.1.call-done = bf16[2048,256]{1,0:T(8,128)(2,1)} async-done(((bf16[256,256]{1,0:T(8,128)(2,1)}), bf16[2048,256]{1,0:T(8,128)(2,1)}) %all-gather.14.cloned.1.call-update) | async-done | bytes 1048592 | tf_op jit(solution)/shard_map/all_gather | solution.py:128
  61.3 82.9 %all-gather.10.cloned.1.call-done = bf16[1024,1,2048]{2,0,1:T(8,128)(2,1)} async-done(((bf16[256,1,2048]{2,0,1:T(8,128)(2,1)}), bf16[1024,1,2048]{2,0,1:T(8,128)(2,1)}) %all-gather.10.cloned.1.call-update) | async-done | bytes 4194320 | tf_op jit(solution)/shard_map/all_gather | solution.py:143
  149.5 22.8 %all-gather.16.cloned.1.call-done = bf16[2048,512]{1,0:T(8,128)(2,1)} async-done(((bf16[256,512]{1,0:T(8,128)(2,1)}), bf16[2048,512]{1,0:T(8,128)(2,1)}) %all-gather.16.cloned.1.call-update) | async-done | bytes 2097168 | tf_op jit(solution)/shard_map/all_gather | solution.py:127
  215.8 76.4 %reduce-scatter.12.cloned.1.call-done = bf16[256,1,2048]{2,0,1:T(8,128)(2,1)} async-done(((bf16[1024,1,2048]{2,0,1:T(8,128)(2,1)}), bf16[256,1,2048]{2,0,1:T(8,128)(2,1)}) %reduce-scatter.12.cloned.1.call-update) | async-done | bytes 1048592 | tf_op jit(solution)/shard_map/reduce_scatter | solution.py:151
  301.7 24.1 %collective-permute-done = bf16[256,1,2048]{2,0,1:T(8,128)(2,1)S(1)} collective-permute-done((bf16[256,1,2048]{2,0,1:T(8,128)(2,1)S(1)}, bf16[256,1,2048]{2,0,1:T(8,128)(2,1)S(1)}, u32[]{:S(2)}, u32[]{:S(2)}) %collective-permute-start) | collective-permute-done | bytes 1048608 | tf_op jit(solution)/shard_map/ppermute | solution.py:23
  325.8 20.1 %collective-permute-start.2 = (bf16[256,1,2048]{2,0,1:T(8,128)(2,1)S(1)}, bf16[256,1,2048]{2,0,1:T(8,128)(2,1)}, u32[]{:S(2)}, u32[]{:S(2)}) collective-permute-start(bf16[256,1,2048]{2,0,1:T(8,128)(2,1)S(1)} %collective-permute-done), channel_id=1, source_target_pairs={{0,1},{1,2},{2,3},{3,0},{4,5},{5,6},{6,7},{7,4},{8,9},{9,10},{10,1... | collective-permute-start | bytes 3145736 | tf_op jit(solution)/shard_map/ppermute | solution.py:23
  352.8 32.4 %collective-permute-done.2 = bf16[256,1,2048]{2,0,1:T(8,128)(2,1)} collective-permute-done((bf16[256,1,2048]{2,0,1:T(8,128)(2,1)S(1)}, bf16[256,1,2048]{2,0,1:T(8,128)(2,1)}, u32[]{:S(2)}, u32[]{:S(2)}) %collective-permute-start.2) | collective-permute-done | bytes 1048608 | tf_op jit(solution)/shard_map/ppermute | solution.py:23
  387.5 49.9 %all-gather.20.cloned.1.call-done = bf16[1024,1,2048]{2,0,1:T(8,128)(2,1)} async-done(((bf16[256,1,2048]{2,0,1:T(8,128)(2,1)}), bf16[1024,1,2048]{2,0,1:T(8,128)(2,1)}) %all-gather.20.cloned.1.call-update) | async-done | bytes 4194320 | tf_op jit(solution)/shard_map/all_gather | solution.py:143
  437.4 11.9 %fusion.13 = f32[1024,1536]{1,0:T(8,128)} fusion(bf16[2048,1536]{1,0:T(8,128)(2,1)} %all-gather.24.cloned.1.call-done, bf16[1024,1,2048]{2,0,1:T(8,128)(2,1)} %all-gather.20.cloned.1.call-done), kind=kOutput, calls=%fused_computation.27 | convolution fusion | flops 6442450944 | bytes 16777216 | tf_op jit(solution)/shard_map/qpt,to->qpo/dot_general | solution.py:251
  449.3 35.0 %all-gather.22.cloned.1.call-done = bf16[2048,1536]{1,0:T(8,128)(2,1)} async-done(((bf16[256,1536]{1,0:T(8,128)(2,1)}), bf16[2048,1536]{1,0:T(8,128)(2,1)}) %all-gather.22.cloned.1.call-update) | async-done | bytes 6291472 | tf_op jit(solution)/shard_map/all_gather | solution.py:136
  484.3 11.7 fusion.15
  496.0 35.4 %all-gather.26.cloned.1.call-done = bf16[2048,1536]{1,0:T(8,128)(2,1)} async-done(((bf16[256,1536]{1,0:T(8,128)(2,1)}), bf16[2048,1536]{1,0:T(8,128)(2,1)}) %all-gather.26.cloned.1.call-update) | async-done | bytes 6291472 | tf_op jit(solution)/shard_map/all_gather | solution.py:138
  531.5 17.3 %multiply_convert_fusion = (bf16[1024,1536]{1,0:T(8,128)(2,1)}, bf16[1024,1536]{1,0:T(8,128)(2,1)}, bf16[1024,1536]{1,0:T(8,128)(2,1)}) fusion(f32[1024,1536]{1,0:T(8,128)} %fusion.15, f32[1024,1536]{1,0:T(8,128)} %fusion.13, bf16[1024,2048]{1,0:T(8,128)(2,1)} %bitcast_dynamic-update-slice_fusion.4, bf16[2048,1536]{1,0:T(8,128)(2,1)} %all-gather.26.cloned.1.call-done), kind=kOutput, calls=%fused_computation.19 | convolution fusion | flops 6466043904 | bytes 32505856 | tf_op jit(solution)/shard_map/qpt,to->qpo/dot_general | solution.py:265
  557.6 11.2 fusion.10
  568.8 11.5 convolution_convert_fusion.2
  580.4 11.7 convolution_convert_fusion.1
  592.1 11.5 convolution_convert_fusion
  603.7 42.0 %reduce-scatter.16.cloned.1.call-done = bf16[256,1,2048]{2,0,1:T(8,128)(2,1)} async-done(((bf16[1024,1,2048]{2,0,1:T(8,128)(2,1)}), bf16[256,1,2048]{2,0,1:T(8,128)(2,1)}) %reduce-scatter.16.cloned.1.call-update) | async-done | bytes 1048592 | tf_op jit(solution)/shard_map/reduce_scatter | solution.py:160
  653.5 24.1 %collective-permute-done.3 = bf16[256,1,2048]{2,0,1:T(8,128)(2,1)S(1)} collective-permute-done((bf16[256,1,2048]{2,0,1:T(8,128)(2,1)S(1)}, bf16[256,1,2048]{2,0,1:T(8,128)(2,1)S(1)}, u32[]{:S(2)}, u32[]{:S(2)}) %collective-permute-start.3) | collective-permute-done | bytes 1048608 | tf_op jit(solution)/shard_map/ppermute | solution.py:23
  677.6 20.3 %collective-permute-start.5 = (bf16[256,1,2048]{2,0,1:T(8,128)(2,1)S(1)}, bf16[256,1,2048]{2,0,1:T(8,128)(2,1)S(1)}, u32[]{:S(2)}, u32[]{:S(2)}) collective-permute-start(bf16[256,1,2048]{2,0,1:T(8,128)(2,1)S(1)} %collective-permute-done.3), channel_id=1, source_target_pairs={{0,1},{1,2},{2,3},{3,0},{4,5},{5,6},{6,7},{7,4},{8,9},{9,10},{10,1... | collective-permute-start | bytes 3145736 | tf_op jit(solution)/shard_map/ppermute | solution.py:23
  699.9 21.2 %collective-permute-done.5 = bf16[256,1,2048]{2,0,1:T(8,128)(2,1)S(1)} collective-permute-done((bf16[256,1,2048]{2,0,1:T(8,128)(2,1)S(1)}, bf16[256,1,2048]{2,0,1:T(8,128)(2,1)S(1)}, u32[]{:S(2)}, u32[]{:S(2)}) %collective-permute-start.5) | collective-permute-done | bytes 1048608 | tf_op jit(solution)/shard_map/ppermute | solution.py:23
  735.0 11.0 fusion.2
  805.4 11.2 convert_bitcast_fusion
  821.8 19.6 %reduce-scatter.32.cloned.1.call-done = bf16[256,1536]{1,0:T(8,128)(2,1)} async-done(((bf16[2048,1536]{1,0:T(8,128)(2,1)}), bf16[256,1536]{1,0:T(8,128)(2,1)}) %reduce-scatter.32.cloned.1.call-update) | async-done | bytes 786448 | tf_op jit(solution)/shard_map/reduce_scatter | solution.py:358
  843.9 36.6 %reduce-scatter.22.cloned.1.call-done = bf16[256,256]{1,0:T(8,128)(2,1)} async-done(((bf16[2048,256]{1,0:T(8,128)(2,1)}), bf16[256,256]{1,0:T(8,128)(2,1)}) %reduce-scatter.22.cloned.1.call-update) | async-done | bytes 131088 | tf_op jit(solution)/shard_map/reduce_scatter | solution.py:343
  882.1 37.4 %reduce-scatter.24.cloned.1.call-done = bf16[256,256]{1,0:T(8,128)(2,1)} async-done(((bf16[2048,256]{1,0:T(8,128)(2,1)}), bf16[256,256]{1,0:T(8,128)(2,1)}) %reduce-scatter.24.cloned.1.call-update) | async-done | bytes 131088 | tf_op jit(solution)/shard_map/reduce_scatter | solution.py:346
  921.1 42.6 %reduce-scatter.26.cloned.1.call-done = bf16[256,512]{1,0:T(8,128)(2,1)} async-done(((bf16[2048,512]{1,0:T(8,128)(2,1)}), bf16[256,512]{1,0:T(8,128)(2,1)}) %reduce-scatter.26.cloned.1.call-update) | async-done | bytes 262160 | tf_op jit(solution)/shard_map/reduce_scatter | solution.py:349
  965.5 42.5 %reduce-scatter.20.cloned.1.call-done = bf16[256,512]{1,0:T(8,128)(2,1)} async-done(((bf16[2048,512]{1,0:T(8,128)(2,1)}), bf16[256,512]{1,0:T(8,128)(2,1)}) %reduce-scatter.20.cloned.1.call-update) | async-done | bytes 262160 | tf_op jit(solution)/shard_map/reduce_scatter | solution.py:340
  1009.8 77.3 %reduce-scatter.18.cloned.1.call-done = bf16[256,1,2048]{2,0,1:T(8,128)(2,1)} async-done(((bf16[1024,1,2048]{2,0,1:T(8,128)(2,1)}), bf16[256,1,2048]{2,0,1:T(8,128)(2,1)}) %reduce-scatter.18.cloned.1.call-update) | async-done | bytes 1048592 | tf_op jit(solution)/shard_map/reduce_scatter | solution.py:160
  1089.2 46.4 %all-reduce = (f32[2048]{0:T(1024)}, f32[128]{0:T(128)}, f32[128]{0:T(128)}, f32[2048]{0:T(1024)}) all-reduce(f32[2048]{0:T(1024)S(1)} %get-tuple-element.17, f32[128]{0:T(128)S(1)} %get-tuple-element.13, f32[128]{0:T(128)S(1)} %get-tuple-element.19, f32[2048]{0:T(1024)S(1)} %get-tuple-element.15), channel_id=1, replica_groups=mesh['dp'=8,'tensor'=4] {'dp','tensor'}, use_global_device_ids=true, to_apply=%region_16.17 | all-reduce | flops 4352 | bytes 34816 | tf_op jit(solution)/shard_map/psum | solution.py:330
  1135.5 32.1 %reduce-scatter.14.cloned.1.call-done = bf16[256,1,2048]{2,0,1:T(8,128)(2,1)} async-done(((bf16[1024,1,2048]{2,0,1:T(8,128)(2,1)}), bf16[256,1,2048]{2,0,1:T(8,128)(2,1)}) %reduce-scatter.14.cloned.1.call-update) | async-done | bytes 1048592 | tf_op jit(solution)/shard_map/reduce_scatter | solution.py:151
  (277 shorter events, 194.0 us)
Async XLA Ops:
  7.2 28.8 %all-gather.12.cloned.1.call-start = ((), (), s32[]{:S(2)}) async-start(), calls=%async_computation.12 | async-start | bytes 1179648 | tf_op jit(solution)/shard_map/all_gather | solution.py:129
  7.9 53.4 %all-gather.14.cloned.1.call-start = ((), (), s32[]{:S(2)}) async-start(), calls=%async_computation.13 | async-start | bytes 1179648 | tf_op jit(solution)/shard_map/all_gather | solution.py:128
  8.7 135.5 %all-gather.10.cloned.1.call-start = ((), (), s32[]{:S(2)}) async-start(), calls=%async_computation.11 | async-start | bytes 5242880 | tf_op jit(solution)/shard_map/all_gather | solution.py:143
  13.5 158.8 %all-gather.16.cloned.1.call-start = ((), (), s32[]{:S(2)}) async-start(), calls=%async_computation.14 | async-start | bytes 2359296 | tf_op jit(solution)/shard_map/all_gather | solution.py:127
  14.1 193.9 %all-gather.18.cloned.1.call-start = ((), (), s32[]{:S(2)}) async-start(), calls=%async_computation.15 | async-start | bytes 2359296 | tf_op jit(solution)/shard_map/all_gather | solution.py:130
  14.7 277.5 %reduce-scatter.12.cloned.1.call-start = ((), (), s32[]{:S(2)}) async-start(), calls=%async_computation.16 | async-start | bytes 5242880 | tf_op jit(solution)/shard_map/reduce_scatter | solution.py:151
  14.8 164.0 %copy-start.53 = (f32[128]{0:T(128)}, f32[128]{0:T(128)S(1)}, u32[]{:S(2)}) copy-start(f32[128]{0:T(128)S(1)} %convert_element_type.240) | copy-start | bytes 1540
  17.5 162.7 %copy-start.51 = (f32[128]{0:T(128)}, f32[128]{0:T(128)S(1)}, u32[]{:S(2)}) copy-start(f32[128]{0:T(128)S(1)} %convert_element_type.242) | copy-start | bytes 1540
  215.0 172.5 %all-gather.24.cloned.1.call-start = ((), (), s32[]{:S(2)}) async-start(), calls=%async_computation.19 | async-start | bytes 7077888 | tf_op jit(solution)/shard_map/all_gather | solution.py:137
  215.7 221.7 %all-gather.20.cloned.1.call-start = ((), (), s32[]{:S(2)}) async-start(), calls=%async_computation.17 | async-start | bytes 5242880 | tf_op jit(solution)/shard_map/all_gather | solution.py:143
  296.4 187.9 %all-gather.22.cloned.1.call-start = ((), (), s32[]{:S(2)}) async-start(), calls=%async_computation.18 | async-start | bytes 7077888 | tf_op jit(solution)/shard_map/all_gather | solution.py:136
  297.2 234.3 %all-gather.26.cloned.1.call-start = ((), (), s32[]{:S(2)}) async-start(), calls=%async_computation.20 | async-start | bytes 7077888 | tf_op jit(solution)/shard_map/all_gather | solution.py:138
  297.8 348.0 %reduce-scatter.16.cloned.1.call-start = ((), (), s32[]{:S(2)}) async-start(), calls=%async_computation.22 | async-start | bytes 5242880 | tf_op jit(solution)/shard_map/reduce_scatter | solution.py:160
  297.8 28.0 %collective-permute-start = (bf16[256,1,2048]{2,0,1:T(8,128)(2,1)S(1)}, bf16[256,1,2048]{2,0,1:T(8,128)(2,1)S(1)}, u32[]{:S(2)}, u32[]{:S(2)}) collective-permute-start(bf16[256,1,2048]{2,0,1:T(8,128)(2,1)S(1)} %copy-done.18), channel_id=1, source_target_pairs={{0,1},{1,2},{2,3},{3,0},{4,5},{5,6},{6,7},{7,4},{8,9},{9,10},{10,1... | collective-permute-start | bytes 3145736 | tf_op jit(solution)/shard_map/ppermute | solution.py:23
  299.4 51.1 %collective-permute-start.1 = (bf16[256,1,2048]{2,0,1:T(8,128)(2,1)S(1)}, bf16[256,1,2048]{2,0,1:T(8,128)(2,1)}, u32[]{:S(2)}, u32[]{:S(2)}) collective-permute-start(bf16[256,1,2048]{2,0,1:T(8,128)(2,1)S(1)} %copy-done.18), channel_id=1, source_target_pairs={{0,3},{1,0},{2,1},{3,2},{4,7},{5,4},{6,5},{7,6},{8,11},{9,8},{10,9... | collective-permute-start | bytes 3145736 | tf_op jit(solution)/shard_map/ppermute | solution.py:26
  325.8 59.4 %collective-permute-start.2 = (bf16[256,1,2048]{2,0,1:T(8,128)(2,1)S(1)}, bf16[256,1,2048]{2,0,1:T(8,128)(2,1)}, u32[]{:S(2)}, u32[]{:S(2)}) collective-permute-start(bf16[256,1,2048]{2,0,1:T(8,128)(2,1)S(1)} %collective-permute-done), channel_id=1, source_target_pairs={{0,1},{1,2},{2,3},{3,0},{4,5},{5,6},{6,7},{7,4},{8,9},{9,10},{10,1... | collective-permute-start | bytes 3145736 | tf_op jit(solution)/shard_map/ppermute | solution.py:23
  568.8 247.9 %reduce-scatter.28.cloned.1.call-start = ((), (), s32[]{:S(2)}) async-start(), calls=%async_computation.28 | async-start | bytes 7077888 | tf_op jit(solution)/shard_map/reduce_scatter | solution.py:352
  580.3 238.8 %reduce-scatter.30.cloned.1.call-start = ((), (), s32[]{:S(2)}) async-start(), calls=%async_computation.29 | async-start | bytes 7077888 | tf_op jit(solution)/shard_map/reduce_scatter | solution.py:355
  592.1 249.3 %reduce-scatter.32.cloned.1.call-start = ((), (), s32[]{:S(2)}) async-start(), calls=%async_computation.30 | async-start | bytes 7077888 | tf_op jit(solution)/shard_map/reduce_scatter | solution.py:358
  603.7 276.8 %reduce-scatter.22.cloned.1.call-start = ((), (), s32[]{:S(2)}) async-start(), calls=%async_computation.25 | async-start | bytes 1179648 | tf_op jit(solution)/shard_map/reduce_scatter | solution.py:343
  649.7 28.0 %collective-permute-start.3 = (bf16[256,1,2048]{2,0,1:T(8,128)(2,1)S(1)}, bf16[256,1,2048]{2,0,1:T(8,128)(2,1)S(1)}, u32[]{:S(2)}, u32[]{:S(2)}) collective-permute-start(bf16[256,1,2048]{2,0,1:T(8,128)(2,1)S(1)} %get-tuple-element.27), channel_id=1, source_target_pairs={{0,1},{1,2},{2,3},{3,0},{4,5},{5,6},{6,7},{7,4},{8,9},{9,10},{10,1... | collective-permute-start | bytes 3145736 | tf_op jit(solution)/shard_map/ppermute | solution.py:23
  651.2 48.6 %collective-permute-start.4 = (bf16[256,1,2048]{2,0,1:T(8,128)(2,1)S(1)}, bf16[256,1,2048]{2,0,1:T(8,128)(2,1)S(1)}, u32[]{:S(2)}, u32[]{:S(2)}) collective-permute-start(bf16[256,1,2048]{2,0,1:T(8,128)(2,1)S(1)} %get-tuple-element.27), channel_id=1, source_target_pairs={{0,3},{1,0},{2,1},{3,2},{4,7},{5,4},{6,5},{7,6},{8,11},{9,8},{10,9... | collective-permute-start | bytes 3145736 | tf_op jit(solution)/shard_map/ppermute | solution.py:26
  677.6 43.5 %collective-permute-start.5 = (bf16[256,1,2048]{2,0,1:T(8,128)(2,1)S(1)}, bf16[256,1,2048]{2,0,1:T(8,128)(2,1)S(1)}, u32[]{:S(2)}, u32[]{:S(2)}) collective-permute-start(bf16[256,1,2048]{2,0,1:T(8,128)(2,1)S(1)} %collective-permute-done.3), channel_id=1, source_target_pairs={{0,1},{1,2},{2,3},{3,0},{4,5},{5,6},{6,7},{7,4},{8,9},{9,10},{10,1... | collective-permute-start | bytes 3145736 | tf_op jit(solution)/shard_map/ppermute | solution.py:23
  758.7 160.8 %reduce-scatter.24.cloned.1.call-start = ((), (), s32[]{:S(2)}) async-start(), calls=%async_computation.26 | async-start | bytes 1179648 | tf_op jit(solution)/shard_map/reduce_scatter | solution.py:346
  771.6 192.1 %reduce-scatter.26.cloned.1.call-start = ((), (), s32[]{:S(2)}) async-start(), calls=%async_computation.27 | async-start | bytes 2359296 | tf_op jit(solution)/shard_map/reduce_scatter | solution.py:349
  777.7 230.3 %reduce-scatter.20.cloned.1.call-start = ((), (), s32[]{:S(2)}) async-start(), calls=%async_computation.24 | async-start | bytes 2359296 | tf_op jit(solution)/shard_map/reduce_scatter | solution.py:340
  796.9 290.2 %reduce-scatter.18.cloned.1.call-start = ((), (), s32[]{:S(2)}) async-start(), calls=%async_computation.23 | async-start | bytes 5242880 | tf_op jit(solution)/shard_map/reduce_scatter | solution.py:160
  805.2 362.5 %reduce-scatter.14.cloned.1.call-start = ((), (), s32[]{:S(2)}) async-start(), calls=%async_computation.21 | async-start | bytes 5242880 | tf_op jit(solution)/shard_map/reduce_scatter | solution.py:151
  816.6 270.5 %copy-start.47 = (f32[2048]{0:T(1024)S(1)}, f32[2048]{0:T(1024)}, u32[]{:S(2)}) copy-start(f32[2048]{0:T(1024)} %copy-done.46) | copy-start | bytes 24580
  816.6 270.5 %copy-start.50 = (f32[256]{0:T(256)S(1)}, f32[256]{0:T(256)}, u32[]{:S(2)}) copy-start(f32[256]{0:T(256)} %copy-done.49) | copy-start | bytes 3076
  819.1 348.5 %copy-start.8 = (bf16[256,1,2048]{2,0,1:T(8,128)(2,1)S(1)}, bf16[256,1,2048]{2,0,1:T(8,128)(2,1)}, u32[]{:S(2)}) copy-start(bf16[256,1,2048]{2,0,1:T(8,128)(2,1)} %reduce-scatter.12.cloned.1.call-done) | copy-start | bytes 3145732
  819.1 348.5 %copy-start.19 = (bf16[256,1,2048]{2,0,1:T(8,128)(2,1)S(1)}, bf16[256,1,2048]{2,0,1:T(8,128)(2,1)}, u32[]{:S(2)}) copy-start(bf16[256,1,2048]{2,0,1:T(8,128)(2,1)} %param.27) | copy-start | bytes 3145732
  (66 other events, 668.8 us)
Sparse Core Ops, SparseCore 0:
  9.9 26.0 all-gather.11
  37.9 23.3 all-gather.13
  63.5 80.7 all-gather.9
  146.0 26.2 all-gather.15
  174.0 27.7 all-gather.17
  215.1 77.0 reduce-scatter.11
  294.1 45.9 all-gather.23
  342.1 95.2 all-gather.19
  439.3 44.9 all-gather.21
  486.0 45.3 all-gather.25
  568.9 76.7 reduce-scatter.15
  649.0 62.2 reduce-scatter.27
  714.6 61.7 reduce-scatter.29
  779.6 61.7 reduce-scatter.31
  844.4 35.9 reduce-scatter.21
  883.5 35.9 reduce-scatter.23
  922.6 41.0 reduce-scatter.25
  966.9 41.0 reduce-scatter.19
  1010.3 76.7 reduce-scatter.17
  1089.3 78.3 reduce-scatter.13
